TPU v7x, 512 devices: a whole 4x8x8 slice. The times are simulated.
512 devices in a mesh: orb: 32 (over x, y), grid: 16 (over z, core).
Axes of the slice: x: 4, y: 8, z: 8, core: 2. Of those that a mesh axis runs over, the one named last changes fastest.
Arguments:
- orbitals: float32 [128, 32, 4096], P('orb', 'grid'), may hold values from -6 to 6
- rotation: float32 [128, 128], replicated, may hold values from -0.5 to 0.5
- tile_list: int32 [64, 2], replicated, may hold values from 0 to 31, as said below
- pair_mask: int32 [128, 128], replicated, may hold values from 0 to 1, as said below
Outputs:
- exchange_term: float32 [128, 32, 4096], P('orb', 'grid')
Inputs may be any that keep to these rules, and one draw needn't show every extreme that they name: `tile_list`: row t names one tile: its target block and its source block of 4 orbitals each; no tile is named twice. `pair_mask`: among the 1024 orbital pairs that lie in listed tiles, exactly 512 are 1.
All inputs are finite; a program needn't handle non-finite values.
Results may differ from a plain program's by a relative error of at most 0.0003.
Values sent between devices are 32-bit elements; how exact they have to be, the bound alone decides.
A program may use at most 64 MiB of HBM per device.

v0:
```python
import jax
import jax.numpy as jnp
from jax import lax
from jax.sharding import PartitionSpec as P

NORB = 128
BLK = 4
NX = 32
NY = 64
NZ = 64
LIVE_DEV = 1
precise = lax.Precision.HIGHEST
coupling = 0.25
screening = 0.1


def split_up(array, dim, devices):
    dims = array.shape
    tiles = array.reshape(*dims[:dim], devices, dims[dim] // devices, *dims[dim + 1 :])
    return jnp.moveaxis(tiles, dim, 0)


def laid_out(tiles, dim):
    dims = list(tiles.shape[1:])
    dims[dim] *= tiles.shape[0]
    return jnp.moveaxis(tiles, 0, dim).reshape(dims)


def joined_exchange(array, axis, axes, splits, concats):
    sizes = [lax.axis_size(a) for a in axes]
    tiles = split_up(array, splits[0], sizes[0])
    tiles = jnp.moveaxis(split_up(tiles, splits[1] + 1, sizes[1]), 0, 1)
    inside = tiles.shape[2:]
    tiles = tiles.reshape(-1, *inside)
    tiles = lax.all_to_all(tiles, axis, split_axis=0, concat_axis=0, tiled=True)
    tiles = laid_out(tiles.reshape(*sizes, *inside), concats[0] + 1)
    return laid_out(tiles, concats[1])


def sine_table(length):
    wave_index = jnp.arange(length, dtype=jnp.float32) + 1.0
    return jnp.sqrt(2.0 / (length + 1.0)) * jnp.sin(
        jnp.pi * wave_index[:, None] * wave_index[None, :] / (length + 1.0)
    )


def eigen_values(length):
    wave_index = jnp.arange(length, dtype=jnp.float32) + 1.0
    return 2.0 - 2.0 * jnp.cos(jnp.pi * wave_index / (length + 1.0))


def green_kernel(size_x, size_y, size_z):
    summed = (
        eigen_values(size_x)[:, None, None]
        + eigen_values(size_y)[None, :, None]
        + eigen_values(size_z)[None, None, :]
    )
    return coupling / (summed + screening)


def pair_lists(tile_list, pair_mask):
    within = jnp.arange(BLK * BLK, dtype=jnp.int32)
    targets = (BLK * tile_list[:, 0:1] + within[None, :] // BLK).reshape(-1)
    sources = (BLK * tile_list[:, 1:2] + within[None, :] % BLK).reshape(-1)
    return (targets, sources, pair_mask[targets, sources])


def compact(targets, sources, live_flags, number):
    ranking = jnp.cumsum(live_flags) - 1
    places = jnp.where(live_flags == 1, ranking, number)
    picked = (
        jnp.zeros((number,), jnp.int32)
        .at[places]
        .set(jnp.arange(live_flags.shape[0], dtype=jnp.int32), mode="drop")
    )
    return (targets[picked], sources[picked])


def along_z(values, matrix):
    number, planes, width_yz = values.shape
    size_z = matrix.shape[0]
    shaped = values.reshape(number, planes, width_yz // size_z, size_z)
    return jnp.einsum("pxrz,zk->pxrk", shaped, matrix, precision=precise).reshape(
        number, planes, width_yz
    )


def along_y(values, matrix):
    number, planes, width_yz = values.shape
    size_y = matrix.shape[0]
    shaped = values.reshape(number, planes, size_y, width_yz // size_y)
    return jnp.einsum("pxyz,yk->pxkz", shaped, matrix, precision=precise).reshape(
        number, planes, width_yz
    )


def along_x(values, matrix):
    return jnp.einsum("pxc,xk->pkc", values, matrix, precision=precise)


def regroup(values, outer, middle):
    return values.reshape(outer, middle, -1).transpose(1, 0, 2).reshape(-1)


def on_device(orbitals, rotation, tile_list, pair_mask):
    rotated = jnp.einsum(
        "ij,ixc->jxc",
        rotation,
        lax.all_to_all(orbitals, "orb", split_axis=2, concat_axis=0, tiled=True),
        precision=precise,
    )
    planes = rotated.shape[1]
    width_yz = rotated.shape[2]
    targets, sources, live_flags = pair_lists(tile_list, pair_mask)
    weights = live_flags.astype(jnp.float32)
    matrix_x = sine_table(NX)
    matrix_y = sine_table(NY)
    matrix_z = sine_table(NZ)
    kernel = green_kernel(NX, NY, NZ).reshape(NX, NY * NZ)
    orbital_ids = jnp.arange(NORB, dtype=jnp.int32)
    targets, sources = compact(
        targets, sources, live_flags, LIVE_DEV * lax.axis_size("orb") * lax.axis_size("grid")
    )
    density = rotated[targets] * rotated[sources]
    number = density.shape[0]
    spectrum = along_z(density, matrix_z)
    spectrum = joined_exchange(spectrum, ("orb", "grid"), ("orb", "grid"), (0, 0), (2, 1))
    spectrum = along_x(along_y(spectrum, matrix_y), matrix_x) * kernel
    spectrum = along_y(along_x(spectrum, matrix_x), matrix_y)
    spectrum = joined_exchange(spectrum, ("orb", "grid"), ("orb", "grid"), (2, 1), (0, 0))
    outer = lax.axis_size("orb")
    middle = lax.axis_size("grid")
    targets = regroup(targets, outer, middle)
    sources = regroup(sources, outer, middle)
    weights = regroup(weights, outer, middle)
    potential = along_z(spectrum, matrix_z)
    products = potential * rotated[sources]
    selector = (targets[None, :] == orbital_ids[:, None]).astype(jnp.float32)
    partial_value = -jnp.dot(
        selector, products.reshape(number, planes * width_yz), precision=precise
    )
    partial_value = partial_value.reshape(NORB, planes, width_yz)
    return lax.all_to_all(partial_value, "orb", split_axis=0, concat_axis=2, tiled=True)


def solution(mesh):
    in_specs = (P("orb", "grid", None), P(), P(), P())
    out_specs = P("orb", "grid", None)
    return jax.shard_map(
        on_device, mesh=mesh, in_specs=in_specs, out_specs=out_specs, check_vma=False
    )
```

profile of v0, /device:TPU:8, one launch (start us, length us, event | category | flops | bytes accessed | tf_op | source)
XLA Modules:
  0.0 161.6 jit_solution(12426053909212209676)
XLA Ops:
  0.0 5.4 %copy.48 = f32[4,2,4096]{0,1,2:T(2,128)} copy(f32[4,2,4096]{2,1,0:T(2,128)} %param.4) | data formatting | bytes 262144 | tf_op args[0]
  5.4 8.6 %reshape.432 = f32[32,1,1024]{2,1,0:T(1,128)} reshape(f32[4096,2,4]{2,1,0:T(2,128)} %bitcast.97) | data formatting | bytes 262144
  14.0 10.2 %all-to-all-start = ((f32[32,1,1024]{2,1,0:T(1,128)}), f32[32,1,1024]{2,1,0:T(1,128)S(1)}, u32[]{:S(2)}, u32[]{:S(2)}) async-start(f32[32,1,1024]{2,1,0:T(1,128)} %reshape.432), calls=%async_computation | async-start | bytes 262144 | tf_op jit(solution)/shard_map/all_to_all | solution.py:109
  24.6 6.8 %gather_fusion = s32[1024]{0:T(1024)S(1)} fusion(s32[128,128]{1,0:T(8,128)S(1)} %copy-done.1, s32[1024]{0:T(1024)S(1)} %bitcast.95), kind=kCustom, calls=%fused_computation | custom fusion | bytes 16384 | tf_op jit(solution)/shard_map/gather | solution.py:65
  32.1 4.3 %scatter_custom_fusion = s32[512]{0:T(512)S(1)} fusion(s32[1024]{0:T(1024)S(1)} %bitcast.114, s32[1024]{0:T(1024)S(1)} %iota.52, s32[]{:T(128)} %constant.64.clone.1), kind=kCustom, calls=%fused_computation.80 | custom fusion | bytes 2052 | tf_op jit(solution)/shard_map/scatter | solution.py:74
  36.4 2.3 %gather_fusion.3 = s32[512]{0:T(512)S(1)} fusion(s32[1024]{0:T(1024)S(1)} %add.263, s32[1024]{0:T(1024)S(1)} %pad_clamp_fusion.3), kind=kCustom, calls=%fused_computation.3 | custom fusion | bytes 6144 | tf_op jit(solution)/shard_map/gather | solution.py:76
  38.7 2.3 %gather_fusion.1 = s32[512]{0:T(512)S(1)} fusion(s32[1024]{0:T(1024)S(1)} %add.248, s32[1024]{0:T(1024)S(1)} %pad_clamp_fusion.3), kind=kCustom, calls=%fused_computation.1 | custom fusion | bytes 6144 | tf_op jit(solution)/shard_map/gather | solution.py:76
  41.6 0.9 reduce.2
  42.5 7.8 %reshape.433 = f32[4096,2,4]{2,1,0:T(2,128)} reshape(f32[32,1024]{1,0:T(8,128)S(1)} %reduce.2) | data formatting | bytes 262144
  50.3 5.2 %copy.49 = f32[4,2,32,128]{3,0,2,1:T(4,128)S(1)} copy(f32[4,2,32,128]{0,1,3,2:T(2,128)} %bitcast.96) | data formatting | bytes 262144 | tf_op jit(solution)/shard_map/all_to_all | solution.py:109
  55.9 2.1 %gather_fusion.2 = f32[512,2,128]{2,1,0:T(2,128)S(1)} fusion(f32[128,2,128]{2,1,0:T(2,128)S(1)} %copy.51, s32[1024]{0:T(1024)S(1)} %pad_clamp_fusion.2), kind=kCustom, calls=%fused_computation.2 | custom fusion | bytes 1050624 | tf_op jit(solution)/shard_map/gather | solution.py:124
  58.0 2.1 %gather_fusion.4 = f32[512,2,128]{2,1,0:T(2,128)S(1)} fusion(f32[128,2,128]{2,1,0:T(2,128)S(1)} %copy.51, s32[1024]{0:T(1024)S(1)} %pad_clamp_fusion.1), kind=kCustom, calls=%fused_computation.4 | custom fusion | bytes 1050624 | tf_op jit(solution)/shard_map/gather | solution.py:124
  61.4 1.0 copy.54
  62.4 20.7 %all-to-all-start.1 = ((f32[512,1,2,128]{3,2,1,0:T(2,128)}), f32[512,1,2,128]{3,2,1,0:T(2,128)S(1)}, u32[]{:S(2)}, u32[]{:S(2)}) async-start(f32[512,1,2,128]{3,2,1,0:T(2,128)} %copy.54), calls=%async_computation.1 | async-start | bytes 1048576 | tf_op jit(solution)/shard_map/all_to_all | solution.py:35
  84.1 20.1 %all-to-all-done.1 = f32[512,1,2,128]{3,2,1,0:T(2,128)S(1)} async-done(((f32[512,1,2,128]{3,2,1,0:T(2,128)}), f32[512,1,2,128]{3,2,1,0:T(2,128)S(1)}, u32[]{:S(2)}, u32[]{:S(2)}) %all-to-all-start.1) | async-done | bytes 524320 | tf_op jit(solution)/shard_map/all_to_all | solution.py:35
  104.6 1.2 convolution_bitcast_fusion.1
  107.3 1.7 %fusion.4 = f32[32,64,64]{2,0,1:T(8,128)S(1)} fusion(f32[64,64,32]{1,0,2:T(8,128)S(1)} %dot_general.38, f32[32]{0:T(128)S(1)} %get-tuple-element.11, f32[32]{0:T(128)S(1)} %get-tuple-element.12), kind=kOutput, calls=%fused_computation.15 | convolution fusion | flops 50334720 | bytes 1048832 | tf_op jit(solution)/shard_map/pxc,xk->pkc/dot_general | solution.py:98
  109.0 1.8 %convolution_bitcast_fusion = f32[1,32,64,64]{3,2,1,0:T(8,128)S(1)} fusion(f32[32,64,64]{2,0,1:T(8,128)S(1)} %fusion.4, f32[64]{0:T(128)S(1)} %get-tuple-element.9, f32[64]{0:T(128)S(1)} %get-tuple-element.10), kind=kOutput, calls=%fused_computation.9 | convolution fusion | flops 100675584 | bytes 1049088 | tf_op jit(solution)/shard_map/pxyz,yk->pxkz/dot_general | solution.py:92
  111.0 1.1 copy.59
  112.1 9.7 %all-to-all-start.2 = ((f32[512,1,2,128]{3,2,1,0:T(2,128)}), f32[512,1,2,128]{3,2,1,0:T(2,128)S(1)}, u32[]{:S(2)}, u32[]{:S(2)}) async-start(f32[512,1,2,128]{3,2,1,0:T(2,128)} %bitcast.30), calls=%async_computation.2 | async-start | bytes 1048576 | tf_op jit(solution)/shard_map/all_to_all | solution.py:35
  122.3 2.1 %gather_fusion.5 = f32[512,2,128]{2,1,0:T(2,128)S(1)} fusion(f32[128,2,128]{2,1,0:T(2,128)S(1)} %copy.51, s32[1024]{0:T(1024)S(1)} %pad_clamp_fusion), kind=kCustom, calls=%fused_computation.5 | custom fusion | bytes 1050624 | tf_op jit(solution)/shard_map/gather | solution.py:137
  124.6 18.3 %all-to-all-done.2 = f32[512,1,2,128]{3,2,1,0:T(2,128)S(1)} async-done(((f32[512,1,2,128]{3,2,1,0:T(2,128)}), f32[512,1,2,128]{3,2,1,0:T(2,128)S(1)}, u32[]{:S(2)}, u32[]{:S(2)}) %all-to-all-start.2) | async-done | bytes 524320 | tf_op jit(solution)/shard_map/all_to_all | solution.py:35
  143.8 1.5 fusion.1
  145.8 15.0 %all_to_all.46 = f32[128,2,128]{2,1,0:T(2,128)S(1)} all-to-all(f32[128,2,128]{2,1,0:T(2,128)S(1)} %reshape.368), channel_id=1, replica_groups=mesh['orb'=32,'grid'=16] {'orb'}, dimensions={0} | all-to-all | bytes 262144 | tf_op jit(solution)/shard_map/all_to_all | solution.py:143
  (69 shorter events, 9.2 us)
Async XLA Ops:
  0.0 55.5 %copy-start = (f32[128,128]{1,0:T(8,128)S(1)}, f32[128,128]{1,0:T(8,128)}, u32[]{:S(2)}) copy-start(f32[128,128]{1,0:T(8,128)} %param.5) | copy-start | bytes 196612
  0.0 24.2 %copy-start.2 = (s32[64,2]{0,1:T(2,128)S(1)}, s32[64,2]{0,1:T(2,128)}, u32[]{:S(2)}) copy-start(s32[64,2]{0,1:T(2,128)} %param.6) | copy-start | bytes 1540
  0.0 24.6 %copy-start.1 = (s32[128,128]{1,0:T(8,128)S(1)}, s32[128,128]{1,0:T(8,128)}, u32[]{:S(2)}) copy-start(s32[128,128]{1,0:T(8,128)} %param.7) | copy-start | bytes 196612
  14.0 27.1 %all-to-all-start = ((f32[32,1,1024]{2,1,0:T(1,128)}), f32[32,1,1024]{2,1,0:T(1,128)S(1)}, u32[]{:S(2)}, u32[]{:S(2)}) async-start(f32[32,1,1024]{2,1,0:T(1,128)} %reshape.432), calls=%async_computation | async-start | bytes 262144 | tf_op jit(solution)/shard_map/all_to_all | solution.py:109
  62.4 41.8 %all-to-all-start.1 = ((f32[512,1,2,128]{3,2,1,0:T(2,128)}), f32[512,1,2,128]{3,2,1,0:T(2,128)S(1)}, u32[]{:S(2)}, u32[]{:S(2)}) async-start(f32[512,1,2,128]{3,2,1,0:T(2,128)} %copy.54), calls=%async_computation.1 | async-start | bytes 1048576 | tf_op jit(solution)/shard_map/all_to_all | solution.py:35
  112.1 30.9 %all-to-all-start.2 = ((f32[512,1,2,128]{3,2,1,0:T(2,128)}), f32[512,1,2,128]{3,2,1,0:T(2,128)S(1)}, u32[]{:S(2)}, u32[]{:S(2)}) async-start(f32[512,1,2,128]{3,2,1,0:T(2,128)} %bitcast.30), calls=%async_computation.2 | async-start | bytes 1048576 | tf_op jit(solution)/shard_map/all_to_all | solution.py:35
where the time goes:
time: 162 us
  local copies, waits for them, and re-layouts  56.7 us (35%)
  starting transfers between devices  40.6 us (25%)
  waiting for transfers between devices  38.4 us (24%)
  blocking collectives  15 us (9%)
  matrix products  8.41 us (5%)
  other arithmetic  2.05 us (1%)
    all_to_all x2, waiting for transfers between devices, joined_exchange(): tiles = lax.all_to_all(tiles, axis, split_axis=0, concat_axis=0, tiled=True)  38.4 us
    all_to_all x2, starting transfers between devices, joined_exchange(): tiles = lax.all_to_all(tiles, axis, split_axis=0, concat_axis=0, tiled=True)  30.5 us
    unnamed x9, local copies, waits for them, and re-layouts  21.8 us
    all_to_all x1, blocking collectives, on_device(): lax.all_to_all(partial_value, 'orb', split_axis=0, concat_axis=2, tiled=T...  15 us
    all_to_all x1, starting transfers between devices, on_device(): lax.all_to_all(orbitals, 'orb', split_axis=2, concat_axis=0, tiled=True)  10.2 us
    gather x1, local copies, waits for them, and re-layouts, pair_lists(): return (targets, sources, pair_mask[targets, sources])  6.8 us
    all_to_all x2, local copies, waits for them, and re-layouts, on_device(): lax.all_to_all(orbitals, 'orb', split_axis=2, concat_axis=0, tiled=True)  5.67 us
    gather x2, local copies, waits for them, and re-layouts, compact(): return (targets[picked], sources[picked])  4.58 us
  transfers between devices with their start and end apart: 3, of which 2 were waited for; matrix products, arithmetic and copies ran while one was open for 13% of the time, Pallas kernels for 0%

commit v1 on v0

--- a/solution.py
+++ b/solution.py
@@ -106,7 +106,12 @@
     rotated = jnp.einsum(
         "ij,ixc->jxc",
         rotation,
-        lax.all_to_all(orbitals, "orb", split_axis=2, concat_axis=0, tiled=True),
+        jnp.concatenate(
+            lax.all_to_all(
+                jnp.stack(jnp.split(orbitals, lax.axis_size("orb"), axis=2)), "orb", 0, 0
+            ),
+            axis=0,
+        ),
         precision=precise,
     )
     planes = rotated.shape[1]

time: 162 us -> 177 us (1.093)
  local copies, waits for them, and re-layouts: 56.7 us -> 71.5 us
    unnamed x9 -> x37, local copies, waits for them, and re-layouts: 21.8 us -> 41 us
    all_to_all x2 -> x0, local copies, waits for them, and re-layouts: 5.67 us -> none  [on_device(): lax.all_to_all(orbitals, 'orb', split_axis=2, concat_axis=0, tiled=True)]
  transfers between devices with their start and end apart: 3 -> 3, of which waited for: 2 -> 2; matrix products, arithmetic and copies ran while one was open for 13% -> 12% of each run, Pallas kernels for 0% -> 0%
where the time goes in v1:
time: 177 us; the launch traced here: 175 us
  local copies, waits for them, and re-layouts  71.5 us (40%)
  starting transfers between devices  40.5 us (23%)
  waiting for transfers between devices  38.3 us (22%)
  blocking collectives  15 us (8%)
  matrix products  8.49 us (5%)
    unnamed x37, local copies, waits for them, and re-layouts  41 us
    all_to_all x2, waiting for transfers between devices, joined_exchange(): tiles = lax.all_to_all(tiles, axis, split_axis=0, concat_axis=0, tiled=True)  38.3 us
    all_to_all x2, starting transfers between devices, joined_exchange(): tiles = lax.all_to_all(tiles, axis, split_axis=0, concat_axis=0, tiled=True)  30.3 us
    all_to_all x1, blocking collectives, on_device(): lax.all_to_all(partial_value, 'orb', split_axis=0, concat_axis=2, tiled=T...  15 us
    all_to_all x1, starting transfers between devices, on_device(): lax.all_to_all(jnp.stack(jnp.split(orbitals, lax.axis_size('orb'), axis=2...  10.2 us
    gather x1, local copies, waits for them, and re-layouts, pair_lists(): return (targets, sources, pair_mask[targets, sources])  6.79 us
    gather x2, local copies, waits for them, and re-layouts, compact(): return (targets[picked], sources[picked])  4.58 us
    scatter x1, local copies, waits for them, and re-layouts, compact(): picked = jnp.zeros((number,), jnp.int32).at[places].set(jnp.arange(live_f...  4.3 us
  transfers between devices with their start and end apart: 3, of which 2 were waited for; matrix products, arithmetic and copies ran while one was open for 12% of the time, Pallas kernels for 0%

profile of v1, /device:TPU:8, one launch (start us, length us, event | category | flops | bytes accessed | tf_op | source)
XLA Modules:
  0.0 175.3 jit_solution(1320229226145944315)
XLA Ops:
  0.0 1.3 constant_dynamic-update-slice_fusion.31
  3.9 1.3 constant_dynamic-update-slice_fusion.28
  7.7 1.3 constant_dynamic-update-slice_fusion.25
  11.6 1.3 constant_dynamic-update-slice_fusion.22
  15.4 1.3 constant_dynamic-update-slice_fusion.19
  30.7 1.3 constant_dynamic-update-slice_fusion.7
  32.0 1.3 constant_dynamic-update-slice_fusion.6
  33.3 1.3 constant_dynamic-update-slice_fusion.5
  41.0 10.2 %all-to-all-start = ((f32[32,4,2,128]{3,2,1,0:T(2,128)}), f32[32,4,2,128]{3,2,1,0:T(2,128)S(1)}, u32[]{:S(2)}, u32[]{:S(2)}) async-start(f32[32,4,2,128]{3,2,1,0:T(2,128)} %constant_dynamic-update-slice_fusion), calls=%async_computation | async-start | bytes 262144 | tf_op jit(solution)/shard_map/all_to_all | solution.py:110
  52.9 6.8 %gather_fusion = s32[1024]{0:T(1024)S(1)} fusion(s32[128,128]{1,0:T(8,128)S(1)} %copy-done.1, s32[1024]{0:T(1024)S(1)} %bitcast.155), kind=kCustom, calls=%fused_computation | custom fusion | bytes 16384 | tf_op jit(solution)/shard_map/gather | solution.py:65
  60.3 4.3 %scatter_custom_fusion = s32[512]{0:T(512)S(1)} fusion(s32[1024]{0:T(1024)S(1)} %bitcast.172, s32[1024]{0:T(1024)S(1)} %iota.52, s32[]{:T(128)} %constant.64.clone.1), kind=kCustom, calls=%fused_computation.113 | custom fusion | bytes 2052 | tf_op jit(solution)/shard_map/scatter | solution.py:74
  64.7 2.3 %gather_fusion.1 = s32[512]{0:T(512)S(1)} fusion(s32[1024]{0:T(1024)S(1)} %add.248, s32[1024]{0:T(1024)S(1)} %pad_clamp_fusion.3), kind=kCustom, calls=%fused_computation.1 | custom fusion | bytes 6144 | tf_op jit(solution)/shard_map/gather | solution.py:76
  67.0 2.3 %gather_fusion.3 = s32[512]{0:T(512)S(1)} fusion(s32[1024]{0:T(1024)S(1)} %add.263, s32[1024]{0:T(1024)S(1)} %pad_clamp_fusion.3), kind=kCustom, calls=%fused_computation.3 | custom fusion | bytes 6144 | tf_op jit(solution)/shard_map/gather | solution.py:76
  69.9 2.1 %gather_fusion.2 = f32[512,2,128]{2,1,0:T(2,128)S(1)} fusion(f32[128,2,128]{2,1,0:T(2,128)S(1)} %copy.45, s32[1024]{0:T(1024)S(1)} %pad_clamp_fusion.2), kind=kCustom, calls=%fused_computation.2 | custom fusion | bytes 1050624 | tf_op jit(solution)/shard_map/gather | solution.py:129
  72.0 2.1 %gather_fusion.4 = f32[512,2,128]{2,1,0:T(2,128)S(1)} fusion(f32[128,2,128]{2,1,0:T(2,128)S(1)} %copy.45, s32[1024]{0:T(1024)S(1)} %pad_clamp_fusion.1), kind=kCustom, calls=%fused_computation.4 | custom fusion | bytes 1050624 | tf_op jit(solution)/shard_map/gather | solution.py:129
  76.4 20.7 %all-to-all-start.1 = ((f32[512,1,2,128]{3,2,1,0:T(2,128)}), f32[512,1,2,128]{3,2,1,0:T(2,128)S(1)}, u32[]{:S(2)}, u32[]{:S(2)}) async-start(f32[512,1,2,128]{3,2,1,0:T(2,128)} %copy.48), calls=%async_computation.1 | async-start | bytes 1048576 | tf_op jit(solution)/shard_map/all_to_all | solution.py:35
  98.1 20.0 %all-to-all-done.1 = f32[512,1,2,128]{3,2,1,0:T(2,128)S(1)} async-done(((f32[512,1,2,128]{3,2,1,0:T(2,128)}), f32[512,1,2,128]{3,2,1,0:T(2,128)S(1)}, u32[]{:S(2)}, u32[]{:S(2)}) %all-to-all-start.1) | async-done | bytes 524320 | tf_op jit(solution)/shard_map/all_to_all | solution.py:35
  121.3 1.7 fusion.4
  122.9 1.8 %convolution_bitcast_fusion = f32[1,32,64,64]{3,2,1,0:T(8,128)S(1)} fusion(f32[32,64,64]{2,0,1:T(8,128)S(1)} %fusion.4, f32[64]{0:T(128)S(1)} %get-tuple-element.9, f32[64]{0:T(128)S(1)} %get-tuple-element.10), kind=kOutput, calls=%fused_computation.9 | convolution fusion | flops 100675584 | bytes 1049088 | tf_op jit(solution)/shard_map/pxyz,yk->pxkz/dot_general | solution.py:92
  126.0 9.6 %all-to-all-start.2 = ((f32[512,1,2,128]{3,2,1,0:T(2,128)}), f32[512,1,2,128]{3,2,1,0:T(2,128)S(1)}, u32[]{:S(2)}, u32[]{:S(2)}) async-start(f32[512,1,2,128]{3,2,1,0:T(2,128)} %bitcast.61), calls=%async_computation.2 | async-start | bytes 1048576 | tf_op jit(solution)/shard_map/all_to_all | solution.py:35
  136.1 2.1 %gather_fusion.5 = f32[512,2,128]{2,1,0:T(2,128)S(1)} fusion(f32[128,2,128]{2,1,0:T(2,128)S(1)} %copy.45, s32[1024]{0:T(1024)S(1)} %pad_clamp_fusion), kind=kCustom, calls=%fused_computation.5 | custom fusion | bytes 1050624 | tf_op jit(solution)/shard_map/gather | solution.py:142
  138.4 18.3 %all-to-all-done.2 = f32[512,1,2,128]{3,2,1,0:T(2,128)S(1)} async-done(((f32[512,1,2,128]{3,2,1,0:T(2,128)}), f32[512,1,2,128]{3,2,1,0:T(2,128)S(1)}, u32[]{:S(2)}, u32[]{:S(2)}) %all-to-all-start.2) | async-done | bytes 524320 | tf_op jit(solution)/shard_map/all_to_all | solution.py:35
  157.5 1.5 fusion.1
  159.6 15.0 %all_to_all.33 = f32[128,2,128]{2,1,0:T(2,128)S(1)} all-to-all(f32[128,2,128]{2,1,0:T(2,128)S(1)} %reshape.372), channel_id=1, replica_groups=mesh['orb'=32,'grid'=16] {'orb'}, dimensions={0} | all-to-all | bytes 262144 | tf_op jit(solution)/shard_map/all_to_all | solution.py:148
  (95 shorter events, 44.0 us)
Async XLA Ops:
  0.0 69.3 %copy-start = (f32[128,128]{1,0:T(8,128)S(1)}, f32[128,128]{1,0:T(8,128)}, u32[]{:S(2)}) copy-start(f32[128,128]{1,0:T(8,128)} %param.5) | copy-start | bytes 196612
  41.0 28.3 %all-to-all-start = ((f32[32,4,2,128]{3,2,1,0:T(2,128)}), f32[32,4,2,128]{3,2,1,0:T(2,128)S(1)}, u32[]{:S(2)}, u32[]{:S(2)}) async-start(f32[32,4,2,128]{3,2,1,0:T(2,128)} %constant_dynamic-update-slice_fusion), calls=%async_computation | async-start | bytes 262144 | tf_op jit(solution)/shard_map/all_to_all | solution.py:110
  51.2 0.7 copy-start.2
  52.1 0.8 copy-start.1
  76.4 41.8 %all-to-all-start.1 = ((f32[512,1,2,128]{3,2,1,0:T(2,128)}), f32[512,1,2,128]{3,2,1,0:T(2,128)S(1)}, u32[]{:S(2)}, u32[]{:S(2)}) async-start(f32[512,1,2,128]{3,2,1,0:T(2,128)} %copy.48), calls=%async_computation.1 | async-start | bytes 1048576 | tf_op jit(solution)/shard_map/all_to_all | solution.py:35
  126.0 30.6 %all-to-all-start.2 = ((f32[512,1,2,128]{3,2,1,0:T(2,128)}), f32[512,1,2,128]{3,2,1,0:T(2,128)S(1)}, u32[]{:S(2)}, u32[]{:S(2)}) async-start(f32[512,1,2,128]{3,2,1,0:T(2,128)} %bitcast.61), calls=%async_computation.2 | async-start | bytes 1048576 | tf_op jit(solution)/shard_map/all_to_all | solution.py:35
